TPU v7x, 32 devices: a whole 2x2x4 slice. The times are simulated.
32 devices in a mesh: dp: 2 (over core), section: 4 (over z), mp: 4 (over y, x).
Axes of the slice: x: 2, y: 2, z: 4, core: 2. Of those that a mesh axis runs over, the one named last changes fastest.
Arguments:
- inputs: bfloat16 [48, 512], P(('dp', 'mp')), may hold values from -6 to 6
- tangents: bfloat16 [48, 32, 512], P(('dp', 'mp')), may hold values from -6 to 6
- targets: bfloat16 [48, 1024], P(('dp', 'mp')), may hold values from -24 to 24
- target_jac: bfloat16 [48, 32, 1024], P(('dp', 'mp')), may hold values from -24 to 24
- rank_mask: int32 [48, 32], P(('dp', 'mp')), may hold values from 0 to 1, as said below
- batch_order: int32 [8, 6], P(('dp', 'mp')), may hold values from 0 to 5, each once within a row
- encoder: bfloat16 [512, 2048], replicated, may hold values from -0.25 to 0.25
- layers: bfloat16 [4, 2048, 2048], P('section', 'mp'), may hold values from -0.125 to 0.125
- head_weight: bfloat16 [2048, 1024], replicated, may hold values from -0.125 to 0.125
Outputs:
- grad_layers: float32 [4, 2048, 2048], P('section', ('dp', 'mp'))
- grad_head: float32 [2048, 1024], P(('dp', 'mp'), 'section')
- loss_value: float32 [], replicated
Inputs may be any that keep to these rules, and one draw needn't show every extreme that they name: `rank_mask`: each sample's ones are its first 1 to 32 directions. `batch_order`: each row is an ordering of 0 .. 5.
All inputs are finite; a program needn't handle non-finite values.
Results may differ from a plain program's by a relative error of at most 0.035.
Values may be sent and summed in bfloat16 or wider, within the bound.
A program may use at most 128 MiB of HBM per device.

v0:
```python
import functools

import jax
import jax.numpy as jnp
from jax import lax
from jax.experimental import pallas as pl
from jax.experimental.pallas import tpu as pltpu
from jax.sharding import PartitionSpec as P

MB = 6


def from_behind(value, axis, steps):
    count = lax.axis_size(axis)
    initial, last = (max(0, -steps), min(count, count - steps))
    return lax.ppermute(value, axis, [(source, source + steps) for source in range(initial, last)])


def forward_layer(row_block, weight):
    model_width = weight.shape[1]
    pre_act = jnp.dot(
        row_block.reshape(-1, model_width), weight, preferred_element_type=jnp.float32
    ).reshape(row_block.shape)
    tanh_p = jnp.tanh(pre_act[:, 0])
    slope_vals = 1.0 - tanh_p * tanh_p
    primal = row_block[:, 0].astype(jnp.float32) + tanh_p
    tangent = row_block[:, 1:].astype(jnp.float32) + slope_vals[:, None, :] * pre_act[:, 1:]
    return (jnp.concatenate([primal[:, None], tangent], axis=1).astype(jnp.bfloat16), pre_act)


def backward_layer(pre_act, grad_rows, weight):
    model_width = weight.shape[1]
    upstream = grad_rows.astype(jnp.float32)
    tanh_p = jnp.tanh(pre_act[:, 0])
    slope_vals = 1.0 - tanh_p * tanh_p
    tangent_part = upstream[:, 1:] * slope_vals[:, None, :]
    slope_grad = jnp.sum(upstream[:, 1:] * pre_act[:, 1:], axis=1)
    primal_part = upstream[:, 0] * slope_vals - 2.0 * slope_grad * tanh_p * slope_vals
    grad_mix = jnp.concatenate([primal_part[:, None], tangent_part], axis=1).astype(jnp.bfloat16)
    back_rows = jnp.dot(
        grad_mix.reshape(-1, model_width), weight.T, preferred_element_type=jnp.float32
    ).reshape(upstream.shape)
    return (grad_mix, (upstream + back_rows).astype(jnp.bfloat16))


def place_slot(store, value, batch_slot, is_valid):
    return lax.dynamic_update_index_in_dim(
        store, jnp.where(is_valid, value, store[batch_slot]), batch_slot, 0
    )


def local(
    inputs, tangents, targets, target_jac, rank_mask, batch_order, encoder, layers, head_weight
):
    samp_dev = inputs.shape[0]
    per_batch = samp_dev // MB
    row_depth = tangents.shape[1] + 1
    in_width = inputs.shape[1]
    model_width = layers.shape[2]
    out_width = head_weight.shape[1]
    sections = lax.axis_size("section")
    section_id = lax.axis_index("section")
    is_first = section_id == 0
    is_last = section_id == sections - 1
    layer_full = lax.all_gather(layers[0], "mp", axis=0, tiled=True)
    sample_order = batch_order[0]
    row_weight = jnp.concatenate(
        [jnp.ones((samp_dev, 1), jnp.float32), rank_mask.astype(jnp.float32)], axis=1
    )
    sample_total = jnp.sum(row_weight, axis=1)
    batch_counts = lax.psum(
        jnp.sum(sample_total[sample_order].reshape(MB, per_batch), axis=1), "mp"
    )

    def picked_of(batch_slot):
        return lax.dynamic_slice_in_dim(sample_order, batch_slot * per_batch, per_batch)

    def lift_batch(batch_slot):
        picked = picked_of(batch_slot)
        rows_in = jnp.concatenate([inputs[picked][:, None, :], tangents[picked]], axis=1)
        lifted = jnp.dot(rows_in.reshape(-1, in_width), encoder, preferred_element_type=jnp.float32)
        return lifted.reshape(per_batch, row_depth, model_width).astype(jnp.bfloat16)

    block_shape = (MB, per_batch, row_depth, model_width)
    pre_shape = (1, 1, 1, 1)

    def forward_tick(step_index, loop_state):
        incoming, store_in, store_pre, store_out = loop_state
        batch_index = step_index - section_id
        is_valid = (batch_index >= 0) & (batch_index < MB)
        batch_slot = jnp.clip(batch_index, 0, MB - 1)
        row_block = lax.cond(is_first, lambda: lift_batch(batch_slot), lambda: incoming)

        def forward_active():
            return forward_layer(row_block, layer_full)

        def forward_resting():
            return (row_block, jnp.zeros(row_block.shape, jnp.float32))

        layer_out, pre_act = lax.cond(is_valid, forward_active, forward_resting)
        store_in = place_slot(store_in, row_block, batch_slot, is_valid)
        store_out = place_slot(store_out, layer_out, batch_slot, is_valid)
        passed = from_behind(layer_out, "section", 1)
        return (passed, store_in, store_pre, store_out)

    start_state = (
        jnp.zeros(block_shape[1:], jnp.bfloat16),
        jnp.zeros(block_shape, jnp.bfloat16),
        jnp.zeros(pre_shape, jnp.float32),
        jnp.zeros(block_shape, jnp.bfloat16),
    )
    _, store_in, store_pre, store_out = lax.fori_loop(
        0, MB + sections - 1, forward_tick, start_state
    )

    def backward_tick(step_index, loop_state):
        incoming, store_mix, store_head, loss_acc = loop_state
        batch_index = step_index - (sections - 1 - section_id)
        is_valid = (batch_index >= 0) & (batch_index < MB)
        batch_slot = jnp.clip(batch_index, 0, MB - 1)
        batch_total = batch_counts[batch_slot]

        def head_part():
            final_rows = store_out[batch_slot]
            outputs = jnp.dot(
                final_rows.reshape(-1, model_width), head_weight, preferred_element_type=jnp.float32
            )
            outputs = outputs.reshape(per_batch, row_depth, out_width)
            picked = picked_of(batch_slot)
            wanted = jnp.concatenate(
                [targets[picked][:, None, :], target_jac[picked]], axis=1
            ).astype(jnp.float32)
            weights_here = row_weight[picked]
            mismatch = outputs - wanted
            misfit = jnp.sum(weights_here[:, :, None] * mismatch * mismatch) / batch_total
            cot_out = (2.0 * weights_here[:, :, None] * mismatch / batch_total).astype(jnp.bfloat16)
            grad_rows = jnp.dot(
                cot_out.reshape(-1, out_width), head_weight.T, preferred_element_type=jnp.float32
            )
            return (
                grad_rows.reshape(per_batch, row_depth, model_width).astype(jnp.bfloat16),
                cot_out,
                misfit,
            )

        def pass_on():
            return (
                incoming,
                jnp.zeros((per_batch, row_depth, out_width), jnp.bfloat16),
                jnp.zeros((), jnp.float32),
            )

        grad_rows, cot_out, misfit = lax.cond(is_last & is_valid, head_part, pass_on)

        def backward_active():
            row_block = store_in[batch_slot]
            pre_act = jnp.dot(
                row_block.reshape(-1, model_width), layer_full, preferred_element_type=jnp.float32
            ).reshape(row_block.shape)
            return backward_layer(pre_act, grad_rows, layer_full)

        def backward_resting():
            return (jnp.zeros(grad_rows.shape, jnp.bfloat16), grad_rows)

        grad_mix, grad_in = lax.cond(is_valid, backward_active, backward_resting)
        store_mix = place_slot(store_mix, grad_mix, batch_slot, is_valid)
        store_head = place_slot(store_head, cot_out, batch_slot, is_valid)
        loss_acc = loss_acc + jnp.where(is_valid, misfit, jnp.zeros((), jnp.float32))
        passed = from_behind(grad_in, "section", -1)
        return (passed, store_mix, store_head, loss_acc)

    back_state = (
        jnp.zeros(block_shape[1:], jnp.bfloat16),
        jnp.zeros(block_shape, jnp.bfloat16),
        jnp.zeros((MB, per_batch, row_depth, out_width), jnp.bfloat16),
        jnp.zeros((), jnp.float32),
    )
    _, store_mix, store_head, loss_acc = lax.fori_loop(
        0, MB + sections - 1, backward_tick, back_state
    )
    shard_rows = model_width // (lax.axis_size("dp") * lax.axis_size("mp"))
    in_flat = store_in.reshape(-1, model_width)
    mix_flat = store_mix.reshape(-1, model_width)
    grad_layers = lax.psum_scatter(
        jnp.dot(in_flat.T, mix_flat, preferred_element_type=jnp.float32).astype(jnp.bfloat16),
        ("dp", "mp"),
        scatter_dimension=0,
        tiled=True,
    ).astype(jnp.float32)[None]
    out_flat = store_out.reshape(-1, model_width)
    head_flat = store_head.reshape(-1, out_width)

    def compute():
        return jnp.dot(out_flat.T, head_flat, preferred_element_type=jnp.float32)

    def skipped():
        return jnp.zeros((lax.axis_size(("dp", "mp")) * shard_rows, out_width), jnp.float32)

    summed = lax.psum_scatter(
        lax.cond(is_last, compute, skipped).astype(jnp.bfloat16),
        ("dp", "mp"),
        scatter_dimension=0,
        tiled=True,
    )
    section_loss = lax.psum(loss_acc, ("dp", "mp"))
    loss_row = jnp.broadcast_to(section_loss, (1, sections))
    grad_head, loss_cols = (
        lax.psum_scatter(summed, "section", scatter_dimension=1, tiled=True).astype(jnp.float32),
        lax.psum_scatter(
            loss_row.astype(jnp.bfloat16), "section", scatter_dimension=1, tiled=True
        ).astype(jnp.float32),
    )
    loss_value = loss_cols[0, 0] / (lax.axis_size("dp") * MB * out_width)
    return (grad_layers, grad_head, loss_value)


MESH = pl.DeviceIdType.MESH
TILE = 512
LANES = 128
SUBLANES = 16


def step_kernel(
    shape,
    shard_ref, enc_ref, head_ref, rows_ref, wanted_ref, mask_ref, count_ref,
    dw_ref, gh_ref, loss_ref,
    w, hin, hout, pre, cot_in, cot_out, mix, hcols, lcols, cotg, gsend, grecv, counts, losses, total, loss_acc,
    w_send, w_recv, f_send, f_recv, b_send, b_recv, m_send, m_recv,
    h_send, h_recv, l_send, l_recv, c_send, c_recv, g_send, g_recv, k_send, k_recv,
    s_send, s_recv, t_send, t_recv,
):
    n_sec, chunks, per, rank, depth = shape
    f32, bf16 = jnp.float32, jnp.bfloat16
    width = w.shape[0]
    out_width = head_ref.shape[1]
    half = width // 2
    tang = per * rank
    n_rows = chunks * depth
    shard = shard_ref.shape[0]
    piece = shard // 2
    cols = hcols.shape[1]
    dp = lax.axis_index("dp")
    sec = lax.axis_index("section")
    mp = lax.axis_index("mp")
    y, x = mp // 2, mp % 2
    is_first = sec == 0
    is_last = sec == n_sec - 1
    mps = (mp, 2 * y + (1 - x), 2 * (1 - y) + x, 2 * (1 - y) + (1 - x))
    dps = (dp, 1 - dp)

    def plane(a, k):
        return (dps[a], sec, mps[k])

    barrier = pltpu.get_barrier_semaphore()
    peers = [(a, k) for a in range(2) for k in range(4) if (a, k) != (0, 0)]
    for a, k in peers:
        pl.semaphore_signal(barrier, inc=1, device_id=plane(a, k), device_id_type=MESH)
    for hop in range(1, n_sec):
        other = (dp, (sec + hop) % n_sec, mp)
        pl.semaphore_signal(barrier, inc=1, device_id=other, device_id_type=MESH)
    pl.semaphore_wait(barrier, len(peers) + n_sec - 1)

    def remote(src, dst, send, recv, to):
        return pltpu.make_async_remote_copy(
            src_ref=src, dst_ref=dst, send_sem=send, recv_sem=recv,
            device_id=to, device_id_type=MESH,
        )

    def spread(own, block, left, right, send, recv):
        acts = {}
        acts["x"] = remote(own, block(0, 0), send(0), recv(0), plane(0, 1))
        acts["y"] = remote(own, block(0, 0), send(1), recv(1), plane(0, 2))
        acts["xy"] = remote(left(0, 1), left(0, 1), send(2), recv(2), plane(0, 2))
        acts["yx"] = remote(right(0, 2), right(0, 2), send(3), recv(3), plane(0, 1))
        for k in range(4):
            src = own if k == 0 else block(0, k)
            acts[k] = remote(src, block(0, k), send(4 + k), recv(4 + k), plane(1, 0))
        return acts

    def w_at(a, k):
        at = pl.multiple_of(mps[k] * shard + dps[a] * piece, piece)
        return w.at[pl.ds(at, piece)]

    def w_left(a, k):
        at = pl.multiple_of(mps[k] * shard + dps[a] * piece, piece)
        return w.at[pl.ds(at, piece), pl.ds(0, half)]

    def w_right(a, k):
        at = pl.multiple_of(mps[k] * shard + dps[a] * piece, piece)
        return w.at[pl.ds(at, piece), pl.ds(half, half)]

    own_w = shard_ref.at[pl.ds(pl.multiple_of(dp * piece, piece), piece)]
    wg = spread(own_w, w_at, w_left, w_right, lambda i: w_send.at[i], lambda i: w_recv.at[i])
    wg["x"].start()
    wg["y"].start()
    w[pl.ds(pl.multiple_of(mp * shard, shard), shard), :] = shard_ref[...]
    loss_acc[...] = jnp.zeros_like(loss_acc)
    place_of = dp * 4 + mp

    def slot(index):
        return pl.ds(pl.multiple_of(index * 8, 8), 8)

    k_acts = [
        remote(
            count_ref, counts.at[slot(k)], k_send.at[k], k_recv.at[k], plane(0, k)
        )
        for k in range(1, 4)
    ]

    @pl.when(is_last)
    def _():
        for act in k_acts:
            act.start()

    @pl.when(is_first)
    def _():
        @pl.loop(0, width // TILE)
        def _(t):
            at = pl.ds(pl.multiple_of(t * TILE, TILE), TILE)
            hin[:, at] = jnp.dot(
                rows_ref[...], enc_ref[:, at], preferred_element_type=f32
            ).astype(bf16)

    def relay(acts):
        acts["x"].wait_recv()
        acts["xy"].start()
        acts[1].start()
        acts["y"].wait_recv()
        acts["yx"].start()
        acts[2].start()

    def finish(acts, own):
        acts["xy"].wait_recv()
        acts["yx"].wait_recv()
        acts[3].start()
        for k in range(4):
            if k > 0 or own:
                acts[k].wait_recv()
                acts[k].wait_send()
        for key in ("x", "y", "xy", "yx"):
            acts[key].wait_send()

    relay(wg)
    finish(wg, False)

    @pl.when(is_last)
    def _():
        for act in k_acts:
            act.wait_recv()
            act.wait_send()
        counts[pl.ds(0, 8), :] = count_ref[...]
        summed = counts[pl.ds(0, 8), :]
        for k in range(1, 4):
            summed = summed + counts[pl.ds(8 * k, 8), :]
        counts[pl.ds(0, 8), :] = 1.0 / summed

    def rows_of(j):
        return pl.ds(pl.multiple_of(j * depth, SUBLANES), depth)

    def f_copy(j):
        return remote(
            hout.at[rows_of(j)], hin.at[rows_of(j)], f_send.at[j], f_recv.at[j],
            (dp, (sec + 1) % n_sec, mp),
        )

    def b_copy(j):
        return remote(
            cot_out.at[rows_of(j)], cot_in.at[rows_of(j)], b_send.at[j], b_recv.at[j],
            (dp, (sec + n_sec - 1) % n_sec, mp),
        )

    def forward(j):
        rows = rows_of(j)

        @pl.loop(0, width // TILE)
        def _(t):
            at = pl.ds(pl.multiple_of(t * TILE, TILE), TILE)
            act = jnp.dot(hin[rows, :], w[:, at], preferred_element_type=f32)
            pre[rows, at] = act
            old = hin[rows, at].astype(f32)
            tanh_p = jnp.tanh(act[tang:])
            slope = 1.0 - tanh_p * tanh_p
            parts = [
                old[i * rank : (i + 1) * rank]
                + slope[i : i + 1] * act[i * rank : (i + 1) * rank]
                for i in range(per)
            ]
            new = jnp.concatenate(parts + [old[tang:] + tanh_p], axis=0)
            hout[rows, at] = new.astype(bf16)

    def head(j):
        rows = rows_of(j)
        coef = jnp.sum(mask_ref[rows, :] * counts[pl.ds(0, 1), :], axis=1, keepdims=True)

        @pl.loop(0, out_width // TILE)
        def _(t):
            at = pl.ds(pl.multiple_of(t * TILE, TILE), TILE)
            got = jnp.dot(hout[rows, :], head_ref[:, at], preferred_element_type=f32)
            miss = got - wanted_ref[rows, at].astype(f32)
            scaled = coef * miss
            cotg[rows, at] = (2.0 * scaled).astype(bf16)
            loss_acc[...] += jnp.sum(scaled * miss, axis=0, keepdims=True)

        @pl.loop(0, width // TILE)
        def _(t):
            at = pl.ds(pl.multiple_of(t * TILE, TILE), TILE)
            cot_in[rows, at] = lax.dot_general(
                cotg[rows, :], head_ref[at, :], (((1,), (1,)), ((), ())),
                preferred_element_type=f32,
            ).astype(bf16)

    def backward(j):
        rows = rows_of(j)

        @pl.loop(0, width // TILE)
        def _(t):
            at = pl.ds(pl.multiple_of(t * TILE, TILE), TILE)
            cot = cot_in[rows, at].astype(f32)
            act = pre[rows, at]
            tanh_p = jnp.tanh(act[tang:])
            slope = 1.0 - tanh_p * tanh_p
            prod = cot[:tang] * act[:tang]
            place = lax.broadcasted_iota(jnp.int32, tanh_p.shape, 0)
            slope_grad = jnp.zeros_like(tanh_p)
            parts = []
            for i in range(per):
                part = slice(i * rank, (i + 1) * rank)
                parts.append(cot[part] * slope[i : i + 1])
                total = jnp.sum(prod[part], axis=0, keepdims=True)
                slope_grad = jnp.where(place == i, total, slope_grad)
            parts.append(cot[tang:] * slope - 2.0 * slope_grad * tanh_p * slope)
            mix[rows, at] = jnp.concatenate(parts, axis=0).astype(bf16)

        acts = mix_acts_of(j)
        acts["x"].start()
        acts["y"].start()
        acts[0].start()

        @pl.when(sec > 0)
        def _():
            @pl.loop(0, width // TILE)
            def _(t):
                at = pl.ds(pl.multiple_of(t * TILE, TILE), TILE)
                back = lax.dot_general(
                    mix[rows, :], w[at, :], (((1,), (1,)), ((), ())),
                    preferred_element_type=f32,
                )
                cot_out[rows, at] = (cot_in[rows, at].astype(f32) + back).astype(bf16)

            b_copy(j).start()

        @pl.when(j > 0)
        def _():
            relay(mix_acts_of(j - 1))

    def slot_copies(buf, send, recv, j, count, lanes):
        def at(a, k):
            return pl.ds(pl.multiple_of((a * 4 + k) * n_rows + j * depth, SUBLANES), count)

        lo, hi = pl.ds(0, lanes // 2), pl.ds(lanes // 2, lanes // 2)
        acts = {
            "x": remote(buf.at[at(0, 0)], buf.at[at(0, 1)], send(0), recv(0), plane(0, 1)),
            "y": remote(buf.at[at(0, 0)], buf.at[at(0, 2)], send(1), recv(1), plane(0, 2)),
            "xy": remote(buf.at[at(0, 1), lo], buf.at[at(0, 3), lo], send(2), recv(2), plane(0, 2)),
            "yx": remote(buf.at[at(0, 2), hi], buf.at[at(0, 3), hi], send(3), recv(3), plane(0, 1)),
        }
        for k in range(4):
            acts[k] = remote(buf.at[at(0, k)], buf.at[at(1, k)], send(4 + k), recv(4 + k), plane(1, 0))
        return acts

    def mix_acts_of(j):
        return slot_copies(
            mix, lambda i: m_send.at[i, j], lambda i: m_recv.at[i, j], j, depth, width
        )

    def column_copies(src, buf, send, recv):
        acts = []
        for a, k in peers:
            at = a * 4 + k
            theirs = pl.ds(pl.multiple_of((dps[a] * 4 + mps[k]) * cols, cols), cols)
            acts.append(
                remote(
                    src.at[:, theirs], buf.at[pl.ds(at * n_rows, n_rows)],
                    send.at[at], recv.at[at], plane(a, k),
                )
            )
        return acts

    own_cols = pl.ds(pl.multiple_of((dp * 4 + mp) * cols, cols), cols)

    @pl.loop(0, chunks)
    def _(j):
        @pl.when(sec > 0)
        def _():
            f_copy(j).wait_recv()

        forward(j)

        @pl.when(sec < n_sec - 1)
        def _():
            f_copy(j).start()

        @pl.when(is_last)
        def _():
            head(j)
            backward(j)

    h_acts = column_copies(hin, hcols, h_send, h_recv)
    for act in h_acts:
        act.start()
    hcols[pl.ds(0, n_rows), :] = hin[:, own_cols]

    @pl.when(is_last)
    def _():
        l_acts = column_copies(hout, lcols, l_send, l_recv)
        for act in l_acts:
            act.start()
        lcols[pl.ds(0, n_rows), :] = hout[:, own_cols]
        acts = slot_copies(
            cotg, lambda i: c_send.at[i], lambda i: c_recv.at[i], 0, n_rows, out_width
        )
        acts["x"].start()
        acts["y"].start()
        acts[0].start()
        mine = jnp.broadcast_to(jnp.sum(loss_acc[...], axis=1, keepdims=True), (8, 128))
        losses[slot(place_of), :] = mine
        s_acts = [
            remote(
                losses.at[slot(place_of)], losses.at[slot(place_of)],
                s_send.at[a * 4 + k], s_recv.at[a * 4 + k], plane(a, k),
            )
            for a, k in peers
        ]
        for act in s_acts:
            act.start()
        relay(mix_acts_of(chunks - 1))
        relay(acts)
        for act in s_acts:
            act.wait_recv()
            act.wait_send()
        whole = losses[pl.ds(0, 8), :]
        for index in range(1, 8):
            whole = whole + losses[pl.ds(index * 8, 8), :]
        total[...] = whole
        for s in range(n_sec - 1):
            remote(total, total, t_send.at[s], t_recv, (dp, s, mp)).start()
        finish(acts, True)
        for act in l_acts:
            act.wait_recv()
            act.wait_send()
        share = out_width // n_sec
        for s in range(n_sec):
            part = lax.dot_general(
                lcols[...], cotg[:, s * share : (s + 1) * share], (((0,), (0,)), ((), ())),
                preferred_element_type=f32,
            )
            if s == n_sec - 1:
                gh_ref[...] = part
            else:
                gsend[s] = part.astype(bf16)
                remote(gsend.at[s], grecv, g_send.at[s], g_recv, (dp, s, mp)).start()

    @pl.when(sec < n_sec - 1)
    def _():
        @pl.loop(0, chunks)
        def _(j):
            b_copy(j).wait_recv()
            backward(j)

        relay(mix_acts_of(chunks - 1))

    @pl.loop(0, chunks)
    def _(j):
        finish(mix_acts_of(j), True)

    for act in h_acts:
        act.wait_recv()
        act.wait_send()

    @pl.loop(0, width // TILE)
    def _(t):
        at = pl.ds(pl.multiple_of(t * TILE, TILE), TILE)
        dw_ref[:, at] = lax.dot_general(
            hcols[...], mix[:, at], (((0,), (0,)), ((), ())), preferred_element_type=f32
        )

    @pl.when(is_last)
    def _():
        for s in range(n_sec - 1):
            remote(gsend.at[s], grecv, g_send.at[s], g_recv, (dp, s, mp)).wait_send()
            remote(total, total, t_send.at[s], t_recv, (dp, s, mp)).wait_send()

    @pl.when(sec < n_sec - 1)
    def _():
        remote(gsend.at[0], grecv, g_send.at[0], g_recv, (dp, sec + 1, mp)).wait_recv()
        gh_ref[...] = grecv[...].astype(f32)
        remote(total, total, t_send.at[0], t_recv, (dp, sec + 1, mp)).wait_recv()

        @pl.loop(0, chunks)
        def _(j):
            f_copy(j).wait_send()

    @pl.when(sec > 0)
    def _():
        @pl.loop(0, chunks)
        def _(j):
            b_copy(j).wait_send()

    loss_ref[...] = total[...]


def fused(
    inputs, tangents, targets, target_jac, rank_mask, batch_order, encoder, layers, head_weight
):
    samples, rank = tangents.shape[:2]
    width = layers.shape[2]
    out_width = head_weight.shape[1]
    n_sec = lax.axis_size("section")
    per = 2 if samples % 2 == 0 else 1
    chunks = samples // per
    tail = -(-per // SUBLANES) * SUBLANES
    depth = per * rank + tail
    n_rows = chunks * depth

    def arrange(primal, tangent):
        lanes = primal.shape[-1]
        first = tangent.reshape(chunks, per * rank, lanes)
        second = jnp.pad(primal.reshape(chunks, per, lanes), ((0, 0), (0, tail - per), (0, 0)))
        return jnp.concatenate([first, second], axis=1).reshape(n_rows, lanes)

    mask = rank_mask.astype(jnp.float32)
    order = batch_order[0]
    per_batch = samples // MB
    lane = jnp.arange(LANES)
    batch_of = jnp.arange(samples) // per_batch
    hit = (order[:, None, None] == jnp.arange(samples)[None, :, None]) & (
        batch_of[:, None, None] == lane[None, None, :]
    )
    member = jnp.sum(hit.astype(jnp.float32), axis=0)
    spread_mask = arrange(member, mask[:, :, None] * member[:, None, :])
    count = jnp.sum(member * (1.0 + jnp.sum(mask, axis=1))[:, None], axis=0)
    count = jnp.broadcast_to(jnp.where(lane < MB, count, 1.0), (8, LANES))
    cols = width // (lax.axis_size("dp") * lax.axis_size("mp"))
    bf16, f32 = jnp.bfloat16, jnp.float32
    dma = pltpu.SemaphoreType.DMA
    vmem = pl.BlockSpec(memory_space=pltpu.VMEM)
    dw, gh, loss = pl.pallas_call(
        functools.partial(step_kernel, (n_sec, chunks, per, rank, depth)),
        out_shape=(
            jax.ShapeDtypeStruct((cols, width), f32),
            jax.ShapeDtypeStruct((cols, out_width // n_sec), f32),
            jax.ShapeDtypeStruct((8, LANES), f32),
        ),
        in_specs=[vmem] * 7,
        out_specs=(vmem,) * 3,
        scratch_shapes=[
            pltpu.VMEM((width, width), bf16),
            pltpu.VMEM((n_rows, width), bf16),
            pltpu.VMEM((n_rows, width), bf16),
            pltpu.VMEM((n_rows, width), f32),
            pltpu.VMEM((n_rows, width), bf16),
            pltpu.VMEM((n_rows, width), bf16),
            pltpu.VMEM((8 * n_rows, width), bf16),
            pltpu.VMEM((8 * n_rows, cols), bf16),
            pltpu.VMEM((8 * n_rows, cols), bf16),
            pltpu.VMEM((8 * n_rows, out_width), bf16),
            pltpu.VMEM((n_sec - 1, cols, out_width // n_sec), bf16),
            pltpu.VMEM((cols, out_width // n_sec), bf16),
            pltpu.VMEM((32, LANES), f32),
            pltpu.VMEM((64, LANES), f32),
            pltpu.VMEM((8, LANES), f32),
            pltpu.VMEM((1, TILE), f32),
            dma((8,)), dma((8,)),
            dma((chunks,)), dma((chunks,)), dma((chunks,)), dma((chunks,)),
            dma((8, chunks)), dma((8, chunks)),
            dma((8,)), dma((8,)), dma((8,)), dma((8,)),
            dma((8,)), dma((8,)),
            dma((n_sec,)), dma,
            dma((4,)), dma((4,)), dma((8,)), dma((8,)), dma((n_sec,)), dma,
        ],
        compiler_params=pltpu.CompilerParams(
            collective_id=0, has_side_effects=True, vmem_limit_bytes=62 * 2**20
        ),
    )(layers[0], encoder, head_weight, arrange(inputs, tangents), arrange(targets, target_jac), spread_mask, count)
    return (dw[None], gh, loss[0, 0] / (lax.axis_size("dp") * MB * out_width))


def solution(mesh):
    in_specs = (
        P(("dp", "mp"), None),
        P(("dp", "mp"), None, None),
        P(("dp", "mp"), None),
        P(("dp", "mp"), None, None),
        P(("dp", "mp"), None),
        P(("dp", "mp"), None),
        P(),
        P("section", "mp", None),
        P(),
    )
    out_specs = (P("section", ("dp", "mp"), None), P(("dp", "mp"), "section"), P())
    square_plane = mesh.shape["dp"] == 2 and mesh.shape["mp"] == 4
    body = fused if square_plane else local
    return jax.shard_map(body, mesh=mesh, in_specs=in_specs, out_specs=out_specs, check_vma=False)
```

profile of v0, /device:TPU:25, one launch (start us, length us, event | category | flops | bytes accessed | tf_op | source)
XLA Modules:
  0.0 182.9 jit_solution(15752901290048477736)
XLA Ops:
  0.6 0.8 convert_reduce_fusion.1
  1.4 0.7 iota_compare_fusion.4
  2.2 0.1 convert_reduce_fusion
  2.3 0.1 multiply_reduce_fusion
  2.4 0.6 broadcast_in_dim.9.count_ref
  3.0 0.7 convert_element_type.12
  3.6 0.1 mul.26
  3.7 0.7 reshape.90
  4.4 0.7 reshape.93
  5.2 0.1 bitcast_multiply_fusion
  5.3 0.7 select_maximum_fusion
  5.9 1.6 fusion.3
  7.6 1.8 fusion.1
  9.4 166.7 %shard_map.112 = (f32[256,2048]{1,0:T(8,128)}, f32[256,256]{1,0:T(8,128)}, f32[8,128]{1,0:T(8,128)}) custom-call(bf16[512,2048]{1,0:T(8,128)(2,1)} %bitcast.12, bf16[512,2048]{1,0:T(8,128)(2,1)} %enc_ref.1, bf16[2048,1024]{1,0:T(8,128)(2,1)} %head_ref.1, bf16[240,512]{1,0:T(8,128)(2,1)} %bitcast.15, bf16[240,1024]{1,0:T(8,128)(2,1)} %bitcast.14, ...), custom_call_target="tpu_custom_call" | custom-call | tf_op jit(solution)/shard_map/pallas_call | solution.py:647
  176.1 1.2 slice.3
  177.9 0.0 copy-start
  177.9 3.2 %copy.14 = f32[1,256,2048]{2,1,0:T(8,128)} copy(f32[1,256,2048]{2,1,0:T(8,128)} %bitcast.13) | data formatting | bytes 4194304
  181.1 0.0 copy-done
  181.1 0.7 copy.15
  (5 shorter events, 0.0 us)
Async XLA Ops:
  177.9 3.2 %copy-start = (f32[256,256]{1,0:T(8,128)S(1)}, f32[256,256]{1,0:T(8,128)}, u32[]{:S(2)}) copy-start(f32[256,256]{1,0:T(8,128)} %get-tuple-element.13) | copy-start | bytes 786436
where the time goes:
time: 185 us; the launch traced here: 183 us
  Pallas kernels  167 us (90%)
  local copies, waits for them, and re-layouts  7.22 us (4%)
  other arithmetic  6.61 us (4%)
  between operations  2.46 us (1%)
    pallas_call x1, Pallas kernels, fused(): pl.pallas_call(functools.partial(step_kernel, (n_sec, chunks, per, rank,...  167 us
    concatenate x3, other arithmetic, arrange(): return jnp.concatenate([first, second], axis=1).reshape(n_rows, lanes)  4.11 us
    unnamed x4, local copies, waits for them, and re-layouts  3.88 us

commit v1 on v0

v1 whole, which is shorter than its diff:
```python
import functools

import jax
import jax.numpy as jnp
from jax import lax
from jax.experimental import pallas as pl
from jax.experimental.pallas import tpu as pltpu
from jax.sharding import PartitionSpec as P

MB = 6


def from_behind(value, axis, steps):
    count = lax.axis_size(axis)
    initial, last = (max(0, -steps), min(count, count - steps))
    return lax.ppermute(value, axis, [(source, source + steps) for source in range(initial, last)])


def forward_layer(row_block, weight):
    model_width = weight.shape[1]
    pre_act = jnp.dot(
        row_block.reshape(-1, model_width), weight, preferred_element_type=jnp.float32
    ).reshape(row_block.shape)
    tanh_p = jnp.tanh(pre_act[:, 0])
    slope_vals = 1.0 - tanh_p * tanh_p
    primal = row_block[:, 0].astype(jnp.float32) + tanh_p
    tangent = row_block[:, 1:].astype(jnp.float32) + slope_vals[:, None, :] * pre_act[:, 1:]
    return (jnp.concatenate([primal[:, None], tangent], axis=1).astype(jnp.bfloat16), pre_act)


def backward_layer(pre_act, grad_rows, weight):
    model_width = weight.shape[1]
    upstream = grad_rows.astype(jnp.float32)
    tanh_p = jnp.tanh(pre_act[:, 0])
    slope_vals = 1.0 - tanh_p * tanh_p
    tangent_part = upstream[:, 1:] * slope_vals[:, None, :]
    slope_grad = jnp.sum(upstream[:, 1:] * pre_act[:, 1:], axis=1)
    primal_part = upstream[:, 0] * slope_vals - 2.0 * slope_grad * tanh_p * slope_vals
    grad_mix = jnp.concatenate([primal_part[:, None], tangent_part], axis=1).astype(jnp.bfloat16)
    back_rows = jnp.dot(
        grad_mix.reshape(-1, model_width), weight.T, preferred_element_type=jnp.float32
    ).reshape(upstream.shape)
    return (grad_mix, (upstream + back_rows).astype(jnp.bfloat16))


def place_slot(store, value, batch_slot, is_valid):
    return lax.dynamic_update_index_in_dim(
        store, jnp.where(is_valid, value, store[batch_slot]), batch_slot, 0
    )


def local(
    inputs, tangents, targets, target_jac, rank_mask, batch_order, encoder, layers, head_weight
):
    samp_dev = inputs.shape[0]
    per_batch = samp_dev // MB
    row_depth = tangents.shape[1] + 1
    in_width = inputs.shape[1]
    model_width = layers.shape[2]
    out_width = head_weight.shape[1]
    sections = lax.axis_size("section")
    section_id = lax.axis_index("section")
    is_first = section_id == 0
    is_last = section_id == sections - 1
    layer_full = lax.all_gather(layers[0], "mp", axis=0, tiled=True)
    sample_order = batch_order[0]
    row_weight = jnp.concatenate(
        [jnp.ones((samp_dev, 1), jnp.float32), rank_mask.astype(jnp.float32)], axis=1
    )
    sample_total = jnp.sum(row_weight, axis=1)
    batch_counts = lax.psum(
        jnp.sum(sample_total[sample_order].reshape(MB, per_batch), axis=1), "mp"
    )

    def picked_of(batch_slot):
        return lax.dynamic_slice_in_dim(sample_order, batch_slot * per_batch, per_batch)

    def lift_batch(batch_slot):
        picked = picked_of(batch_slot)
        rows_in = jnp.concatenate([inputs[picked][:, None, :], tangents[picked]], axis=1)
        lifted = jnp.dot(rows_in.reshape(-1, in_width), encoder, preferred_element_type=jnp.float32)
        return lifted.reshape(per_batch, row_depth, model_width).astype(jnp.bfloat16)

    block_shape = (MB, per_batch, row_depth, model_width)
    pre_shape = (1, 1, 1, 1)

    def forward_tick(step_index, loop_state):
        incoming, store_in, store_pre, store_out = loop_state
        batch_index = step_index - section_id
        is_valid = (batch_index >= 0) & (batch_index < MB)
        batch_slot = jnp.clip(batch_index, 0, MB - 1)
        row_block = lax.cond(is_first, lambda: lift_batch(batch_slot), lambda: incoming)

        def forward_active():
            return forward_layer(row_block, layer_full)

        def forward_resting():
            return (row_block, jnp.zeros(row_block.shape, jnp.float32))

        layer_out, pre_act = lax.cond(is_valid, forward_active, forward_resting)
        store_in = place_slot(store_in, row_block, batch_slot, is_valid)
        store_out = place_slot(store_out, layer_out, batch_slot, is_valid)
        passed = from_behind(layer_out, "section", 1)
        return (passed, store_in, store_pre, store_out)

    start_state = (
        jnp.zeros(block_shape[1:], jnp.bfloat16),
        jnp.zeros(block_shape, jnp.bfloat16),
        jnp.zeros(pre_shape, jnp.float32),
        jnp.zeros(block_shape, jnp.bfloat16),
    )
    _, store_in, store_pre, store_out = lax.fori_loop(
        0, MB + sections - 1, forward_tick, start_state
    )

    def backward_tick(step_index, loop_state):
        incoming, store_mix, store_head, loss_acc = loop_state
        batch_index = step_index - (sections - 1 - section_id)
        is_valid = (batch_index >= 0) & (batch_index < MB)
        batch_slot = jnp.clip(batch_index, 0, MB - 1)
        batch_total = batch_counts[batch_slot]

        def head_part():
            final_rows = store_out[batch_slot]
            outputs = jnp.dot(
                final_rows.reshape(-1, model_width), head_weight, preferred_element_type=jnp.float32
            )
            outputs = outputs.reshape(per_batch, row_depth, out_width)
            picked = picked_of(batch_slot)
            wanted = jnp.concatenate(
                [targets[picked][:, None, :], target_jac[picked]], axis=1
            ).astype(jnp.float32)
            weights_here = row_weight[picked]
            mismatch = outputs - wanted
            misfit = jnp.sum(weights_here[:, :, None] * mismatch * mismatch) / batch_total
            cot_out = (2.0 * weights_here[:, :, None] * mismatch / batch_total).astype(jnp.bfloat16)
            grad_rows = jnp.dot(
                cot_out.reshape(-1, out_width), head_weight.T, preferred_element_type=jnp.float32
            )
            return (
                grad_rows.reshape(per_batch, row_depth, model_width).astype(jnp.bfloat16),
                cot_out,
                misfit,
            )

        def pass_on():
            return (
                incoming,
                jnp.zeros((per_batch, row_depth, out_width), jnp.bfloat16),
                jnp.zeros((), jnp.float32),
            )

        grad_rows, cot_out, misfit = lax.cond(is_last & is_valid, head_part, pass_on)

        def backward_active():
            row_block = store_in[batch_slot]
            pre_act = jnp.dot(
                row_block.reshape(-1, model_width), layer_full, preferred_element_type=jnp.float32
            ).reshape(row_block.shape)
            return backward_layer(pre_act, grad_rows, layer_full)

        def backward_resting():
            return (jnp.zeros(grad_rows.shape, jnp.bfloat16), grad_rows)

        grad_mix, grad_in = lax.cond(is_valid, backward_active, backward_resting)
        store_mix = place_slot(store_mix, grad_mix, batch_slot, is_valid)
        store_head = place_slot(store_head, cot_out, batch_slot, is_valid)
        loss_acc = loss_acc + jnp.where(is_valid, misfit, jnp.zeros((), jnp.float32))
        passed = from_behind(grad_in, "section", -1)
        return (passed, store_mix, store_head, loss_acc)

    back_state = (
        jnp.zeros(block_shape[1:], jnp.bfloat16),
        jnp.zeros(block_shape, jnp.bfloat16),
        jnp.zeros((MB, per_batch, row_depth, out_width), jnp.bfloat16),
        jnp.zeros((), jnp.float32),
    )
    _, store_mix, store_head, loss_acc = lax.fori_loop(
        0, MB + sections - 1, backward_tick, back_state
    )
    shard_rows = model_width // (lax.axis_size("dp") * lax.axis_size("mp"))
    in_flat = store_in.reshape(-1, model_width)
    mix_flat = store_mix.reshape(-1, model_width)
    grad_layers = lax.psum_scatter(
        jnp.dot(in_flat.T, mix_flat, preferred_element_type=jnp.float32).astype(jnp.bfloat16),
        ("dp", "mp"),
        scatter_dimension=0,
        tiled=True,
    ).astype(jnp.float32)[None]
    out_flat = store_out.reshape(-1, model_width)
    head_flat = store_head.reshape(-1, out_width)

    def compute():
        return jnp.dot(out_flat.T, head_flat, preferred_element_type=jnp.float32)

    def skipped():
        return jnp.zeros((lax.axis_size(("dp", "mp")) * shard_rows, out_width), jnp.float32)

    summed = lax.psum_scatter(
        lax.cond(is_last, compute, skipped).astype(jnp.bfloat16),
        ("dp", "mp"),
        scatter_dimension=0,
        tiled=True,
    )
    section_loss = lax.psum(loss_acc, ("dp", "mp"))
    loss_row = jnp.broadcast_to(section_loss, (1, sections))
    grad_head, loss_cols = (
        lax.psum_scatter(summed, "section", scatter_dimension=1, tiled=True).astype(jnp.float32),
        lax.psum_scatter(
            loss_row.astype(jnp.bfloat16), "section", scatter_dimension=1, tiled=True
        ).astype(jnp.float32),
    )
    loss_value = loss_cols[0, 0] / (lax.axis_size("dp") * MB * out_width)
    return (grad_layers, grad_head, loss_value)


MESH = pl.DeviceIdType.MESH
TILE = 512
LANES = 128
SUBLANES = 16
PIECES = 4


def cuts_of(tang):
    weights = (2, 2, 1, 1)
    unit = tang // sum(weights)
    if unit % SUBLANES:
        return [(0, tang)]
    cuts, at = [], 0
    for weight in weights:
        cuts.append((at, at + weight * unit))
        at += weight * unit
    return cuts


def step_kernel(
    shape,
    shard_hbm, enc_hbm, head_hbm, tan_hbm, tjac_hbm, inp_ref, tgt_ref, mask_ref, order_ref,
    dw_ref, gh_ref, loss_ref,
    w, wt, enc, head, headt, tan, tjac, inp, tgt, hin, hout, pre, th, sacc, cot_in, cot_out, mix,
    hcols, lcols, cotg, gsend, grecv, counts, losses, total, loss_acc, coef,
    ld, w_send, w_recv, f_send, f_recv, b_send, b_recv, m_send, m_recv,
    h_send, h_recv, l_send, l_recv, c_send, c_recv, g_send, g_recv, k_send, k_recv,
    s_send, s_recv, t_send, t_recv,
):
    n_sec, samples, rank, prim, cuts = shape
    f32, bf16 = jnp.float32, jnp.bfloat16
    width = w.shape[0]
    out_width = head.shape[1]
    half = width // 2
    tang = samples * rank
    n_rows = tang + prim
    last = len(cuts) - 1
    shard = width // 4
    piece = shard // 2
    part = piece // PIECES
    cols = hcols.shape[1]
    dp = lax.axis_index("dp")
    sec = lax.axis_index("section")
    mp = lax.axis_index("mp")
    y, x = mp // 2, mp % 2
    is_first = sec == 0
    is_last = sec == n_sec - 1
    mps = (mp, 2 * y + (1 - x), 2 * (1 - y) + x, 2 * (1 - y) + (1 - x))
    dps = (dp, 1 - dp)
    peers = [(a, k) for a in range(2) for k in range(4) if (a, k) != (0, 0)]

    def plane(a, k):
        return (dps[a], sec, mps[k])

    barrier = pltpu.get_barrier_semaphore()
    for a, k in peers:
        pl.semaphore_signal(barrier, inc=1, device_id=plane(a, k), device_id_type=MESH)
    for hop in range(1, n_sec):
        other = (dp, (sec + hop) % n_sec, mp)
        pl.semaphore_signal(barrier, inc=1, device_id=other, device_id_type=MESH)

    own_rows = pl.ds(pl.multiple_of(mp * shard, shard), shard)
    load_w = pltpu.make_async_copy(shard_hbm, w.at[own_rows], ld.at[0])
    load_enc = pltpu.make_async_copy(enc_hbm, enc, ld.at[1])
    load_tan = pltpu.make_async_copy(tan_hbm, tan, ld.at[2])
    load_head = pltpu.make_async_copy(head_hbm, head, ld.at[3])
    load_tjac = pltpu.make_async_copy(tjac_hbm, tjac, ld.at[4])
    load_w.start()

    @pl.when(is_first)
    def _():
        load_enc.start()
        load_tan.start()

    @pl.when(is_last)
    def _():
        load_head.start()
        load_tjac.start()

    def remote(src, dst, send, recv, to):
        return pltpu.make_async_remote_copy(
            src_ref=src, dst_ref=dst, send_sem=send, recv_sem=recv,
            device_id=to, device_id_type=MESH,
        )

    def w_acts(s):
        def at(k):
            return pl.ds(pl.multiple_of(mps[k] * shard + dp * piece + s * part, part), part)

        lo, hi = pl.ds(0, half), pl.ds(half, half)
        acts = {
            "x": remote(w.at[at(0)], w.at[at(0)], w_send.at[s, 0], w_recv.at[s, 0], plane(0, 1)),
            "y": remote(w.at[at(0)], w.at[at(0)], w_send.at[s, 1], w_recv.at[s, 1], plane(0, 2)),
            "xy": remote(w.at[at(1), lo], w.at[at(1), lo], w_send.at[s, 2], w_recv.at[s, 2], plane(0, 2)),
            "yx": remote(w.at[at(2), hi], w.at[at(2), hi], w_send.at[s, 3], w_recv.at[s, 3], plane(0, 1)),
        }
        for k in range(1, 4):
            acts[k] = remote(w.at[at(k)], w.at[at(k)], w_send.at[s, 4 + k], w_recv.at[s, 4 + k], plane(1, 0))
        return acts

    def relay(acts):
        acts["x"].wait_recv()
        acts["xy"].start()
        acts[1].start()
        acts["y"].wait_recv()
        acts["yx"].start()
        acts[2].start()

    def close(acts):
        acts["xy"].wait_recv()
        acts["yx"].wait_recv()
        acts[3].start()

    def settle(acts, own):
        for k in range(0 if own else 1, 4):
            acts[k].wait_recv()
            acts[k].wait_send()
        for key in ("x", "y", "xy", "yx"):
            acts[key].wait_send()

    pl.semaphore_wait(barrier, len(peers) + n_sec - 1)
    load_w.wait()
    wg = [w_acts(s) for s in range(PIECES)]
    for acts in wg:
        acts["x"].start()
        acts["y"].start()

    def slot(index):
        return pl.ds(pl.multiple_of(index * 8, 8), 8)

    k_acts = [
        remote(counts.at[slot(0)], counts.at[slot(k)], k_send.at[k], k_recv.at[k], plane(0, k))
        for k in range(1, 4)
    ]
    per_batch = samples // MB
    place_of = dp * 4 + mp

    @pl.when(is_last)
    def _():
        mask = mask_ref[...].astype(f32)
        order = order_ref[...]
        lane = lax.broadcasted_iota(jnp.int32, (samples, LANES), 1)
        row = lax.broadcasted_iota(jnp.int32, (samples, LANES), 0)
        member = jnp.zeros((samples, LANES), f32)
        for p in range(samples):
            hit = (order[0:1, p : p + 1] == row) & (lane == p // per_batch)
            member = member + jnp.where(hit, 1.0, 0.0)
        weight = 1.0 + jnp.sum(mask, axis=1, keepdims=True)
        count = jnp.sum(member * weight, axis=0, keepdims=True)
        count = jnp.where(lane[0:1] < MB, count, 1.0)
        counts[pl.ds(0, 8), :] = jnp.broadcast_to(count, (8, LANES))
        for act in k_acts:
            act.start()
        tgt[...] = jnp.zeros_like(tgt)
        tgt[pl.ds(0, samples), :] = tgt_ref[...]
        loss_acc[...] = jnp.zeros_like(loss_acc)
        for act in k_acts:
            act.wait_recv()
            act.wait_send()
        summed = counts[pl.ds(0, 8), :]
        for k in range(1, 4):
            summed = summed + counts[pl.ds(8 * k, 8), :]
        scale = jnp.sum(member * (1.0 / summed[0:1]), axis=1, keepdims=True)
        coef[pl.ds(0, prim), :] = jnp.zeros((prim, LANES), f32)
        coef[pl.ds(0, samples), :] = jnp.broadcast_to(scale, (samples, LANES))
        eye = lax.broadcasted_iota(jnp.int32, (rank, rank), 0) == lax.broadcasted_iota(
            jnp.int32, (rank, rank), 1
        )
        for i in range(samples):
            picked = jnp.where(eye, jnp.broadcast_to(mask[i : i + 1], (rank, rank)), 0.0)
            column = jnp.sum(picked, axis=1, keepdims=True) * scale[i : i + 1]
            coef[pl.ds(prim + i * rank, rank), :] = jnp.broadcast_to(column, (rank, LANES))

    @pl.when(is_first)
    def _():
        inp[...] = jnp.zeros_like(inp)
        inp[pl.ds(0, samples), :] = inp_ref[...]
        load_enc.wait()
        load_tan.wait()
        for t in range(width // TILE):
            at = pl.ds(t * TILE, TILE)
            hin[pl.ds(0, prim), at] = jnp.dot(
                inp[...], enc[:, at], preferred_element_type=f32
            ).astype(bf16)
            hin[pl.ds(prim, tang), at] = jnp.dot(
                tan[...], enc[:, at], preferred_element_type=f32
            ).astype(bf16)

    sacc[...] = jnp.zeros_like(sacc)

    def flip(dst, src):
        block = 512

        @pl.loop(0, src.shape[0] // block)
        def _(r):
            for c in range(src.shape[1] // block):
                rows = pl.ds(pl.multiple_of(r * block, block), block)
                at = pl.ds(c * block, block)
                dst[at, rows] = src[rows, at].T

    @pl.when(is_last)
    def _():
        load_head.wait()
        load_tjac.wait()
        flip(headt, head)

    for acts in wg:
        relay(acts)
    for acts in wg:
        close(acts)
    for acts in wg:
        settle(acts, False)

    @pl.when(jnp.logical_not(is_first))
    def _():
        flip(wt, w)

    def f_rows(j):
        start, stop = cuts[j]
        return (0, stop + prim) if j == 0 else (start + prim, stop + prim)

    def b_rows(j):
        start, stop = cuts[j]
        return (start, tang + prim) if j == last else (start, stop)

    def span(ends):
        return pl.ds(ends[0], ends[1] - ends[0])

    def f_copy(j):
        return remote(
            hout.at[span(f_rows(j))], hin.at[span(f_rows(j))], f_send.at[j], f_recv.at[j],
            (dp, (sec + 1) % n_sec, mp),
        )

    def b_copy(j):
        return remote(
            cot_out.at[span(b_rows(j))], cot_in.at[span(b_rows(j))], b_send.at[j], b_recv.at[j],
            (dp, (sec + n_sec - 1) % n_sec, mp),
        )

    def pieces_of(start, stop):
        while start < stop:
            i = start // rank
            end = min(stop, (i + 1) * rank)
            yield i, start, end
            start = end

    def forward(j):
        start, stop = cuts[j]
        rows = span(f_rows(j))
        skip = prim if j == 0 else 0
        for t in range(width // TILE):
            at = pl.ds(t * TILE, TILE)
            act = jnp.dot(hin[rows, :], w[:, at], preferred_element_type=f32)
            if j == 0:
                top = pl.ds(0, prim)
                tanh_p = jnp.tanh(act[:prim])
                th[:, at] = tanh_p
                hout[top, at] = (hin[top, at].astype(f32) + tanh_p).astype(bf16)
            else:
                tanh_p = th[:, at]
            slope = 1.0 - tanh_p * tanh_p
            for i, lo, hi in pieces_of(start, stop):
                mine = act[skip + lo - start : skip + hi - start]
                pre[pl.ds(lo, hi - lo), at] = mine
                here = pl.ds(prim + lo, hi - lo)
                old = hin[here, at].astype(f32)
                hout[here, at] = (old + slope[i : i + 1] * mine).astype(bf16)

    def head_of(j):
        start, stop = cuts[j]
        ends = f_rows(j)
        rows = span(ends)
        first = 8 * ends[0]
        group = pl.ds(first, ends[1] - ends[0])
        scale = coef[rows, :][:, 0:1]
        for t in range(out_width // TILE):
            at = pl.ds(t * TILE, TILE)
            got = jnp.dot(hout[rows, :], head[:, at], preferred_element_type=f32)
            want = tjac[pl.ds(start, stop - start), at]
            if j == 0:
                want = jnp.concatenate([tgt[:, at], want], axis=0)
            miss = got - want.astype(f32)
            scaled = scale * miss
            cotg[group, at] = (2.0 * scaled).astype(bf16)
            loss_acc[...] += jnp.sum(scaled * miss, axis=0, keepdims=True)
        for t in range(width // TILE):
            at = pl.ds(t * TILE, TILE)
            back = jnp.dot(cotg[group, :], headt[:, at], preferred_element_type=f32).astype(bf16)
            if j == 0:
                cot_in[pl.ds(tang, prim), at] = back[:prim]
                cot_in[pl.ds(start, stop - start), at] = back[prim:]
            else:
                cot_in[pl.ds(start, stop - start), at] = back

    def backward(j):
        start, stop = cuts[j]
        ends = b_rows(j)
        base = 8 * ends[0]
        for t in range(width // TILE):
            at = pl.ds(t * TILE, TILE)
            tanh_p = th[:, at]
            slope = 1.0 - tanh_p * tanh_p
            for i, lo, hi in pieces_of(start, stop):
                cot = cot_in[pl.ds(lo, hi - lo), at].astype(f32)
                mix[pl.ds(base + lo - start, hi - lo), at] = (cot * slope[i : i + 1]).astype(bf16)
                sacc[pl.ds(i, 1), at] += jnp.sum(
                    cot * pre[pl.ds(lo, hi - lo), at], axis=0, keepdims=True
                )
            if j == last:
                cot = cot_in[pl.ds(tang, prim), at].astype(f32)
                top = cot * slope - 2.0 * sacc[:, at] * tanh_p * slope
                mix[pl.ds(base + stop - start, prim), at] = top.astype(bf16)

        @pl.when(sec > 0)
        def _():
            rows = pl.ds(base, ends[1] - ends[0])
            for t in range(width // TILE):
                at = pl.ds(t * TILE, TILE)
                back = jnp.dot(mix[rows, :], wt[:, at], preferred_element_type=f32)
                cot_out[span(ends), at] = (cot_in[span(ends), at].astype(f32) + back).astype(bf16)
            b_copy(j).start()

    def slot_copies(buf, send, recv, first, count, lanes):
        def at(a, k):
            return pl.ds(first + (a * 4 + k) * count, count)

        lo, hi = pl.ds(0, lanes // 2), pl.ds(lanes // 2, lanes // 2)
        acts = {
            "x": remote(buf.at[at(0, 0)], buf.at[at(0, 1)], send(0), recv(0), plane(0, 1)),
            "y": remote(buf.at[at(0, 0)], buf.at[at(0, 2)], send(1), recv(1), plane(0, 2)),
            "xy": remote(buf.at[at(0, 1), lo], buf.at[at(0, 3), lo], send(2), recv(2), plane(0, 2)),
            "yx": remote(buf.at[at(0, 2), hi], buf.at[at(0, 3), hi], send(3), recv(3), plane(0, 1)),
        }
        for k in range(4):
            acts[k] = remote(buf.at[at(0, k)], buf.at[at(1, k)], send(4 + k), recv(4 + k), plane(1, 0))
        return acts

    def open_slots(acts):
        acts["x"].start()
        acts["y"].start()
        acts[0].start()

    def mix_acts(j):
        start, stop = b_rows(j)
        return slot_copies(
            mix, lambda i: m_send.at[i, j], lambda i: m_recv.at[i, j], 8 * start, stop - start, width
        )

    def cotg_acts(j):
        start, stop = f_rows(j)
        return slot_copies(
            cotg, lambda i: c_send.at[i, j], lambda i: c_recv.at[i, j],
            8 * start, stop - start, out_width,
        )

    own_cols = pl.ds(pl.multiple_of(place_of * cols, cols), cols)

    def column_copies(src, rows, buf, first, stride, send, recv):
        acts = []
        for a, k in peers:
            at = a * 4 + k
            theirs = pl.ds(pl.multiple_of((dps[a] * 4 + mps[k]) * cols, cols), cols)
            acts.append(
                remote(
                    src.at[rows, theirs], buf.at[pl.ds(first + at * stride, rows.size)],
                    send.at[at], recv.at[at], plane(a, k),
                )
            )
        return acts

    def h_parts(j):
        start, stop = cuts[j]
        ends = b_rows(j)
        stride = ends[1] - ends[0]
        parts = [(j, pl.ds(prim + start, stop - start), 8 * ends[0], stride)]
        if j == last:
            parts.append((j + 1, pl.ds(0, prim), 8 * ends[0] + stop - start, stride))
        return parts

    def h_acts(j):
        acts = []
        for index, rows, first, stride in h_parts(j):
            acts += column_copies(
                hin, rows, hcols, first, stride, h_send.at[index], h_recv.at[index]
            )
        return acts

    def h_own(j):
        for _, rows, first, _ in h_parts(j):
            hcols[pl.ds(first, rows.size), :] = hin[rows, own_cols]

    def l_acts(j):
        start, stop = f_rows(j)
        return column_copies(
            hout, pl.ds(start, stop - start), lcols, 8 * start, stop - start,
            l_send.at[j], l_recv.at[j],
        )

    def grad(j):
        start, stop = b_rows(j)
        group = pl.ds(8 * start, 8 * (stop - start))
        for t in range(width // TILE):
            at = pl.ds(t * TILE, TILE)
            part = lax.dot_general(
                hcols[group, :], mix[group, at], (((0,), (0,)), ((), ())),
                preferred_element_type=f32,
            )
            if j == 0:
                dw_ref[:, at] = part
            else:
                dw_ref[:, at] += part

    def finish_mix(j):
        acts = mix_acts(j)
        close(acts)
        settle(acts, True)

    def finish_cols(j):
        for act in h_acts(j):
            act.wait_recv()
            act.wait_send()

    chunks = range(len(cuts))
    for j in chunks:
        @pl.when(jnp.logical_not(is_first))
        def _():
            f_copy(j).wait_recv()

        forward(j)

        @pl.when(jnp.logical_not(is_last))
        def _():
            f_copy(j).start()
            for act in h_acts(j):
                act.start()
            h_own(j)

        @pl.when(is_last)
        def _():
            head_of(j)
            open_slots(cotg_acts(j))
            for act in l_acts(j):
                act.start()
            backward(j)
            if j > 0:
                relay(cotg_acts(j - 1))
            start, stop = f_rows(j)
            lcols[pl.ds(8 * start, stop - start), :] = hout[pl.ds(start, stop - start), own_cols]

    @pl.when(is_last)
    def _():
        relay(cotg_acts(last))
        for j in chunks:
            open_slots(mix_acts(j))
        for j in chunks:
            for act in h_acts(j):
                act.start()
            h_own(j)
        mine = jnp.broadcast_to(jnp.sum(loss_acc[...], axis=1, keepdims=True), (8, LANES))
        losses[slot(place_of), :] = mine
        s_acts = [
            remote(
                losses.at[slot(place_of)], losses.at[slot(place_of)],
                s_send.at[a * 4 + k], s_recv.at[a * 4 + k], plane(a, k),
            )
            for a, k in peers
        ]
        for act in s_acts:
            act.start()
        for j in chunks:
            close(cotg_acts(j))
        for j in chunks:
            settle(cotg_acts(j), True)
            for act in l_acts(j):
                act.wait_recv()
                act.wait_send()
        share = out_width // n_sec
        for s in range(n_sec):
            got = lax.dot_general(
                lcols[...], cotg[:, s * share : (s + 1) * share], (((0,), (0,)), ((), ())),
                preferred_element_type=f32,
            )
            if s == n_sec - 1:
                gh_ref[...] = got
            else:
                gsend[s] = got.astype(bf16)
                remote(gsend.at[s], grecv, g_send.at[s], g_recv, (dp, s, mp)).start()
        for act in s_acts:
            act.wait_recv()
            act.wait_send()
        whole = losses[pl.ds(0, 8), :]
        for index in range(1, 8):
            whole = whole + losses[pl.ds(index * 8, 8), :]
        total[...] = whole
        for s in range(n_sec - 1):
            remote(total, total, t_send.at[s], t_recv, (dp, s, mp)).start()
        for j in chunks:
            relay(mix_acts(j))
        for j in chunks:
            finish_mix(j)
            finish_cols(j)
            grad(j)
        for s in range(n_sec - 1):
            remote(gsend.at[s], grecv, g_send.at[s], g_recv, (dp, s, mp)).wait_send()
            remote(total, total, t_send.at[s], t_recv, (dp, s, mp)).wait_send()

    @pl.when(jnp.logical_not(is_last))
    def _():
        for j in chunks:
            b_copy(j).wait_recv()
            backward(j)
            open_slots(mix_acts(j))
            if j > 0:
                relay(mix_acts(j - 1))
            if j > 1:
                finish_mix(j - 2)
                finish_cols(j - 2)
                grad(j - 2)
        relay(mix_acts(last))
        for j in (last - 1, last):
            if j >= 0:
                finish_mix(j)
                finish_cols(j)
                grad(j)
        remote(gsend.at[0], grecv, g_send.at[0], g_recv, (dp, sec + 1, mp)).wait_recv()
        gh_ref[...] = grecv[...].astype(f32)
        remote(total, total, t_send.at[0], t_recv, (dp, sec + 1, mp)).wait_recv()
        for j in chunks:
            f_copy(j).wait_send()

    @pl.when(jnp.logical_not(is_first))
    def _():
        for j in chunks:
            b_copy(j).wait_send()

    loss_ref[...] = total[...]


def fused(
    inputs, tangents, targets, target_jac, rank_mask, batch_order, encoder, layers, head_weight
):
    samples, rank = tangents.shape[:2]
    in_width = inputs.shape[1]
    width = layers.shape[2]
    out_width = head_weight.shape[1]
    n_sec = lax.axis_size("section")
    prim = -(-samples // SUBLANES) * SUBLANES
    tang = samples * rank
    n_rows = tang + prim
    cuts = cuts_of(tang)
    n = len(cuts)
    cols = width // (lax.axis_size("dp") * lax.axis_size("mp"))
    bf16, f32 = jnp.bfloat16, jnp.float32
    dma = pltpu.SemaphoreType.DMA
    vmem = pl.BlockSpec(memory_space=pltpu.VMEM)
    hbm = pl.BlockSpec(memory_space=pl.ANY)
    dw, gh, loss = pl.pallas_call(
        functools.partial(step_kernel, (n_sec, samples, rank, prim, cuts)),
        out_shape=(
            jax.ShapeDtypeStruct((cols, width), f32),
            jax.ShapeDtypeStruct((cols, out_width // n_sec), f32),
            jax.ShapeDtypeStruct((8, LANES), f32),
        ),
        in_specs=[hbm] * 5 + [vmem] * 4,
        out_specs=(vmem,) * 3,
        scratch_shapes=[
            pltpu.VMEM((width, width), bf16),
            pltpu.VMEM((width, width), bf16),
            pltpu.VMEM((in_width, width), bf16),
            pltpu.VMEM((width, out_width), bf16),
            pltpu.VMEM((out_width, width), bf16),
            pltpu.VMEM((tang, in_width), bf16),
            pltpu.VMEM((tang, out_width), bf16),
            pltpu.VMEM((prim, in_width), bf16),
            pltpu.VMEM((prim, out_width), bf16),
            pltpu.VMEM((n_rows, width), bf16),
            pltpu.VMEM((n_rows, width), bf16),
            pltpu.VMEM((tang, width), f32),
            pltpu.VMEM((prim, width), f32),
            pltpu.VMEM((prim, width), f32),
            pltpu.VMEM((n_rows, width), bf16),
            pltpu.VMEM((n_rows, width), bf16),
            pltpu.VMEM((8 * n_rows, width), bf16),
            pltpu.VMEM((8 * n_rows, cols), bf16),
            pltpu.VMEM((8 * n_rows, cols), bf16),
            pltpu.VMEM((8 * n_rows, out_width), bf16),
            pltpu.VMEM((n_sec - 1, cols, out_width // n_sec), bf16),
            pltpu.VMEM((cols, out_width // n_sec), bf16),
            pltpu.VMEM((32, LANES), f32),
            pltpu.VMEM((64, LANES), f32),
            pltpu.VMEM((8, LANES), f32),
            pltpu.VMEM((1, TILE), f32),
            pltpu.VMEM((n_rows, LANES), f32),
            dma((5,)), dma((PIECES, 8)), dma((PIECES, 8)),
            dma((n,)), dma((n,)), dma((n,)), dma((n,)),
            dma((8, n)), dma((8, n)),
            dma((n + 1, 8)), dma((n + 1, 8)), dma((n, 8)), dma((n, 8)),
            dma((8, n)), dma((8, n)),
            dma((n_sec,)), dma,
            dma((4,)), dma((4,)), dma((8,)), dma((8,)), dma((n_sec,)), dma,
        ],
        compiler_params=pltpu.CompilerParams(
            collective_id=0, has_side_effects=True, vmem_limit_bytes=62 * 2**20
        ),
    )(
        layers[0], encoder, head_weight, tangents.reshape(tang, in_width),
        target_jac.reshape(tang, out_width), inputs, targets, rank_mask, batch_order,
    )
    return (dw[None], gh, loss[0, 0] / (lax.axis_size("dp") * MB * out_width))


def solution(mesh):
    in_specs = (
        P(("dp", "mp"), None),
        P(("dp", "mp"), None, None),
        P(("dp", "mp"), None),
        P(("dp", "mp"), None, None),
        P(("dp", "mp"), None),
        P(("dp", "mp"), None),
        P(),
        P("section", "mp", None),
        P(),
    )
    out_specs = (P("section", ("dp", "mp"), None), P(("dp", "mp"), "section"), P())
    square_plane = mesh.shape["dp"] == 2 and mesh.shape["mp"] == 4
    body = fused if square_plane else local
    return jax.shard_map(body, mesh=mesh, in_specs=in_specs, out_specs=out_specs, check_vma=False)
```

time: 185 us -> 152 us (0.82)
  Pallas kernels: 167 us -> 144 us
  other arithmetic: 6.61 us -> 0 us
  local copies, waits for them, and re-layouts: 7.22 us -> 5.08 us
    pallas_call x1, Pallas kernels: 167 us -> 144 us  [fused(): pl.pallas_call(functools.partial(step_kernel, (n_sec, samples, rank, prim...]
    concatenate x3 -> x0, other arithmetic: 4.11 us -> none  [arrange(): return jnp.concatenate([first, second], axis=1).reshape(n_rows, lanes)]
where the time goes in v1:
time: 152 us
  Pallas kernels  144 us (95%)
  local copies, waits for them, and re-layouts  5.08 us (3%)
  between operations  2.43 us (2%)
    pallas_call x1, Pallas kernels, fused(): pl.pallas_call(functools.partial(step_kernel, (n_sec, samples, rank, prim...  144 us
    unnamed x4, local copies, waits for them, and re-layouts  3.88 us

profile of v1, /device:TPU:25, one launch (start us, length us, event | category | flops | bytes accessed | tf_op | source)
XLA Modules:
  0.0 151.7 jit_solution(8365410952808523411)
XLA Ops:
  0.6 144.2 %shard_map.112 = (f32[256,2048]{1,0:T(8,128)}, f32[256,256]{1,0:T(8,128)}, f32[8,128]{1,0:T(8,128)}) custom-call(bf16[512,2048]{1,0:T(8,128)(2,1)} %bitcast.5, bf16[512,2048]{1,0:T(8,128)(2,1)} %enc_hbm.1, bf16[2048,1024]{1,0:T(8,128)(2,1)} %head_hbm.1, bf16[192,512]{1,0:T(8,128)(2,1)} %bitcast.8, bf16[192,1024]{1,0:T(8,128)(2,1)} %bitcast.7, ...), custom_call_target="tpu_custom_call" | custom-call | tf_op jit(solution)/shard_map/pallas_call | solution.py:774
  144.9 1.2 slice.3
  146.7 0.0 copy-start
  146.7 3.2 %copy.14 = f32[1,256,2048]{2,1,0:T(8,128)} copy(f32[1,256,2048]{2,1,0:T(8,128)} %bitcast.6) | data formatting | bytes 4194304
  149.9 0.0 copy-done
  149.9 0.7 copy.15
Async XLA Ops:
  146.7 3.2 %copy-start = (f32[256,256]{1,0:T(8,128)S(1)}, f32[256,256]{1,0:T(8,128)}, u32[]{:S(2)}) copy-start(f32[256,256]{1,0:T(8,128)} %get-tuple-element.13) | copy-start | bytes 786436
